TPU v7x, 32 devices: a whole 2x2x4 slice. The times are simulated.
32 devices in a mesh: gx: 8 (over z, x), gy: 4 (over y, core).
Axes of the slice: x: 2, y: 2, z: 4, core: 2. Of those that a mesh axis runs over, the one named last changes fastest.
Arguments:
- velocity: float32 [2, 1024, 1024], P(None, 'gy', 'gx'), may hold values from -3 to 3
- stress: float32 [3, 1024, 1024], P(None, 'gy', 'gx'), may hold values from -3 to 3
- ice_mass: float32 [1024, 1024], P('gy', 'gx'), may hold values from 0.5 to 4
- strength: float32 [1024, 1024], P('gy', 'gx'), may hold values from 0.2 to 2
- land_mask: int32 [1024, 1024], P('gy', 'gx'), may hold values from 0 to 1
- ocean_forcing: float32 [4, 1024, 1024], P(None, ('gy', 'gx')), may hold values from -3 to 3
Outputs:
- velocity_out: float32 [2, 1024, 1024], P(None, 'gy', 'gx')
- stress_out: float32 [3, 1024, 1024], P(None, 'gy', 'gx')
- residuals: float32 [4], replicated
- ocean_stress: float32 [2, 1024, 1024], P(None, ('gy', 'gx'))
All inputs are finite; a program needn't handle non-finite values.
Results may differ from a plain program's by a relative error of at most 0.0001.
Values sent between devices are 32-bit elements; how exact they have to be, the bound alone decides.
A program may use at most 64 MiB of HBM per device.

v0:
```python
import functools

import jax
import jax.numpy as jnp
from jax import lax
from jax.experimental import pallas as pl
from jax.experimental.pallas import tpu as pltpu
from jax.sharding import PartitionSpec as P

ITERS = 4
DEEP = 8
PAD = 16
LANES = 128
CHUNK = 16
MESH = pl.DeviceIdType.MESH
SW, SE, NW, NE = range(4)


def kernel(
    G, Y, R, C, B,
    vel_in, sig_in, mass_in, strength_in, mask_in, forcing_in,
    vel_out, sig_out, res_out, os_out,
    vel, sig, raw_sig, raw_mass, raw_strength, raw_mask, pull, inv_mass, ice, base, force, edge_force, cor,
    bands, ocean, low, high, corner_out, corner_in, strip, f_out, f_in, sums, partial_y, partial_x,
    in_sem, f_send, f_recv, h_send, h_recv, y_send, y_recv, p_send, p_recv, o_sem, r_send, r_recv,
):
    gx = lax.axis_index("gx")
    gy = lax.axis_index("gy")
    f32 = jnp.float32
    T = PAD + R

    def at(dx, dy):
        return {"gx": lax.rem(gx + dx + G, G), "gy": lax.rem(gy + dy + Y, Y)}

    def remote(src, dst, send, recv, where):
        return pltpu.make_async_remote_copy(
            src_ref=src, dst_ref=dst, send_sem=send, recv_sem=recv, device_id=where, device_id_type=MESH
        )

    def settle(ref, sem):
        pltpu.make_async_copy(ref, ref, sem).wait()

    barrier = pltpu.get_barrier_semaphore()
    partners = [(d, 0) for d in range(1, G)] + [(0, d) for d in range(1, Y)]
    partners += [(dx, dy) for dx in (-1, 1) for dy in (-1, 1)]
    for dx, dy in partners:
        pl.semaphore_signal(barrier, inc=1, device_id=at(dx, dy), device_id_type=MESH)
    inner = pl.ds(PAD, R)
    loads = [
        pltpu.make_async_copy(forcing_in, bands, in_sem.at[0]),
        pltpu.make_async_copy(vel_in, vel.at[:, 0, inner], in_sem.at[1]),
        pltpu.make_async_copy(sig_in, raw_sig.at[:, inner], in_sem.at[2]),
        pltpu.make_async_copy(mass_in, raw_mass.at[inner], in_sem.at[3]),
        pltpu.make_async_copy(strength_in, raw_strength.at[inner], in_sem.at[4]),
        pltpu.make_async_copy(mask_in, raw_mask.at[inner], in_sem.at[5]),
    ]
    for copy in loads:
        copy.start()

    under, over = pl.ds(PAD - DEEP, DEEP), pl.ds(T, DEEP)
    lane8 = lax.broadcasted_iota(jnp.int32, (DEEP, LANES), 1)

    def outside(rows, slot, corners):
        for c in range(2):
            vel[c, 0, rows] = jnp.zeros((DEEP, C), f32)
        for c in range(3):
            raw_sig[c, rows] = jnp.zeros((DEEP, C), f32)
        raw_mass[rows] = jnp.ones((DEEP, C), f32)
        raw_strength[rows] = jnp.zeros((DEEP, C), f32)
        raw_mask[rows] = jnp.zeros((DEEP, C), jnp.int32)
        for c in range(4):
            force[c, rows] = jnp.zeros((DEEP, C), f32)
        f_in[slot] = jnp.zeros((2 * DEEP, LANES), f32)
        for c in corners:
            corner_in[c] = jnp.where(lane8 // (2 * DEEP) == 5, 1.0, 0.0)

    has_south, has_north = gy > 0, gy < Y - 1
    pl.when(jnp.logical_not(has_south))(lambda: outside(under, 0, (SW, SE)))
    pl.when(jnp.logical_not(has_north))(lambda: outside(over, G + 1, (NW, NE)))

    for ref in (vel, sig):
        for c in range(ref.shape[0]):
            for w in range(2):
                for r in (0, T + DEEP):
                    ref[c, w, r : r + DEEP] = jnp.zeros((DEEP, C), f32)
    for n in range(PAD - DEEP, T + DEEP, DEEP):
        lat = (gy * R + (n - PAD) + lax.broadcasted_iota(jnp.int32, (DEEP, C), 0)).astype(f32)
        cor[n : n + DEEP] = 0.3 + 1.2 * (lat + 0.5) / (R * Y)

    loads[0].wait()
    for c in range(G):
        t = bands[:, :, c * C : (c + 1) * C].reshape(4 * B, C).T
        f_out[(c + 1) % G, 0:DEEP, 0 : 4 * B] = t[C - DEEP : C]
        f_out[(c + G - 1) % G, DEEP : 2 * DEEP, 0 : 4 * B] = t[0:DEEP]
    f_in[gx + 1] = f_out[gx]
    own_columns = pl.ds(pl.multiple_of(gx * C, C), C)
    mine = pl.ds(pl.multiple_of(gx * B, B), B)
    padded_mine = pl.ds(pl.multiple_of(PAD + gx * B, DEEP), B)
    force[:, padded_mine] = bands[:, :, own_columns]
    for copy in loads[1:]:
        copy.wait()
    fields = [vel.at[0, 0], vel.at[1, 0], raw_sig.at[0], raw_sig.at[1], raw_sig.at[2], raw_mass, raw_strength, raw_mask]
    west_tile = jnp.zeros((DEEP, LANES), f32)
    east_tile = jnp.zeros((DEEP, LANES), f32)
    for q, field in enumerate(fields):
        t = field[PAD:T, :].astype(f32).T
        lo, hi = t[0:DEEP], t[C - DEEP : C]
        low[q] = lo
        high[q] = hi
        spot = lane8 // (2 * DEEP) == q
        turn = 2 * DEEP * q + DEEP

        def corner(rows):
            both = jnp.where(lane8 < DEEP, rows[:, 0:LANES], rows[:, R - LANES : R])
            return pltpu.roll(both, turn, 1)

        west_tile = jnp.where(spot, corner(lo), west_tile)
        east_tile = jnp.where(spot, corner(hi), east_tile)
    corner_out[0] = west_tile
    corner_out[1] = east_tile

    pl.semaphore_wait(barrier, len(partners))
    low_half = gx < G // 2

    def others(j):
        down = G - 1 - j
        down = down - (down <= gx).astype(jnp.int32)
        return jnp.where(low_half, down, j + (j >= gx).astype(jnp.int32))

    def forcing_sends(js):
        for j in js:
            to = others(j)
            where = {"gx": to, "gy": gy}
            columns = pl.ds(pl.multiple_of(to * C, C), C)
            remote(bands.at[:, :, columns], force.at[:, padded_mine], f_send.at[0], f_recv.at[gx], where).start()
            remote(f_out.at[to], f_in.at[gx + 1], f_send.at[1], f_recv.at[gx], where).start()

    near, far = pl.ds(0, DEEP), pl.ds(DEEP, DEEP)
    centre = pl.ds(LANES, R)
    bottom, top = pl.ds(PAD, DEEP), pl.ds(T - DEEP, DEEP)
    stacks = (vel, raw_sig, raw_mass, raw_strength, raw_mask)

    def rows_of(ref, rows):
        if ref is vel:
            return ref.at[:, 0, rows]
        return ref.at[:, rows] if len(ref.shape) == 3 else ref.at[rows]

    forcing_sends(range(2))
    sides = [
        remote(low, strip.at[:, far, centre], h_send.at[0], h_recv.at[0], at(-1, 0)),
        remote(high, strip.at[:, near, centre], h_send.at[1], h_recv.at[1], at(1, 0)),
    ]
    south = [
        remote(corner_out.at[0], corner_in.at[NE], h_send.at[2], h_recv.at[2], at(-1, -1)),
        remote(corner_out.at[1], corner_in.at[NW], h_send.at[3], h_recv.at[3], at(1, -1)),
    ]
    north = [
        remote(corner_out.at[0], corner_in.at[SE], h_send.at[4], h_recv.at[4], at(-1, 1)),
        remote(corner_out.at[1], corner_in.at[SW], h_send.at[5], h_recv.at[5], at(1, 1)),
    ]
    for copy in sides:
        copy.start()

    @pl.when(has_south)
    def _():
        for copy in south:
            copy.start()
        for ref in stacks:
            remote(rows_of(ref, bottom), rows_of(ref, over), y_send.at[0], y_recv.at[0], at(0, -1)).start()

    @pl.when(has_north)
    def _():
        for copy in north:
            copy.start()
        for ref in stacks:
            remote(rows_of(ref, top), rows_of(ref, under), y_send.at[1], y_recv.at[1], at(0, 1)).start()

    forcing_sends(range(2, G - 1))

    chunks = [(n, CHUNK) for n in range(PAD, T, CHUNK)]
    skirts = [(PAD - DEEP, DEEP), (T, DEEP)]

    def prepare(w, p, n, s0, s1, s2, mass, strength, mask):
        ice[w, p : p + n] = mask
        pull[w, p : p + n] = 0.25 * strength * mask
        inv_mass[w, p : p + n] = 1.0 / mass
        sig[0, w, p : p + n] = (s0 + s1) * mask
        sig[1, w, p : p + n] = (s0 - s1) * mask
        sig[2, w, p : p + n] = 2.0 * s2 * mask

    def prepare_main(p, n):
        rows = pl.ds(p, n)
        prepare(
            0, p, n, raw_sig[0, rows], raw_sig[1, rows], raw_sig[2, rows],
            raw_mass[rows], raw_strength[rows], raw_mask[rows].astype(f32),
        )

    for p, n in chunks:
        prepare_main(p, n)
    pack8 = pl.ds(0, 8 * DEEP)

    @pl.when(has_north)
    def _():
        settle(cor.at[pack8], y_recv.at[0])
        for copy in south:
            copy.wait_recv()

    @pl.when(has_south)
    def _():
        settle(cor.at[pack8], y_recv.at[1])
        for copy in north:
            copy.wait_recv()

    for copy in sides:
        copy.wait_recv()
    for p, n in skirts:
        prepare_main(p, n)
    for q in range(8):
        turn = LANES - (2 * DEEP * q + DEEP)
        for side, (s, n) in ((near, (SW, NW)), (far, (SE, NE))):
            strip[q, side, 0:LANES] = pltpu.roll(corner_in[s], turn, 1)
            strip[q, side, LANES + R : 2 * LANES + R] = pltpu.roll(corner_in[n], turn, 1)
    for tile in range(R // LANES + 2):
        t = strip[:, :, tile * LANES : (tile + 1) * LANES].reshape(8 * 2 * DEEP, LANES).T
        if tile == 0:
            t, p = t[LANES - DEEP :], PAD - DEEP
        elif tile == R // LANES + 1:
            t, p = t[:DEEP], T
        else:
            p = PAD + (tile - 1) * LANES
        for r in range(0, t.shape[0], CHUNK):
            part = t[r : r + CHUNK]
            n = part.shape[0]
            turned = [pltpu.roll(part, LANES - (2 * DEEP * q + DEEP), 1) for q in range(8)]
            vel[0, 1, p + r : p + r + n] = turned[0]
            vel[1, 1, p + r : p + r + n] = turned[1]
            prepare(1, p + r, n, *turned[2:])

    def shifted(a, b, lane):
        ra, rb = pltpu.roll(a, C - 1, 1), pltpu.roll(b, C - 1, 1)
        la, lb = pltpu.roll(a, 1, 1), pltpu.roll(b, 1, 1)
        right, left = lane == C - 1, lane == 0
        return (
            jnp.where(right, rb, ra) - jnp.where(left, lb, la),
            jnp.where(right, ra, rb) - jnp.where(left, la, lb),
        )

    everywhere = skirts[:1] + chunks + skirts[1:]

    def stress_step(last):
        for p, n in everywhere:
            lane = lax.broadcasted_iota(jnp.int32, (n, C), 1)
            rows = pl.ds(p, n)
            dxu = shifted(vel[0, 0, rows], vel[0, 1, rows], lane)
            dxv = shifted(vel[1, 0, rows], vel[1, 1, rows], lane)
            for w in range(2):
                dyu = vel[0, w, p + 1 : p + n + 1] - vel[0, w, p - 1 : p + n - 1]
                dyv = vel[1, w, p + 1 : p + n + 1] - vel[1, w, p - 1 : p + n - 1]
                div = dxu[w] + dyv
                ten = dxu[w] - dyv
                shear = dyu + dxv[w]
                inv = lax.rsqrt(div * div + 0.25 * (ten * ten + shear * shear) + 0.01)
                hold = pull[w, rows]
                scaled = hold * inv
                quarter = 0.25 * scaled
                spread = scaled * div - hold
                twist = quarter * ten
                xx = 0.75 * sig[0, w, rows] + (spread + twist)
                yy = 0.75 * sig[1, w, rows] + (spread - twist)
                xy = 0.75 * sig[2, w, rows] + quarter * shear
                sig[0, w, rows] = xx
                sig[1, w, rows] = yy
                sig[2, w, rows] = xy
                if last and w == 0 and PAD <= p < T:
                    sig_out[0, p - PAD : p - PAD + n] = 0.5 * (xx + yy)
                    sig_out[1, p - PAD : p - PAD + n] = 0.5 * (xx - yy)
                    sig_out[2, p - PAD : p - PAD + n] = 0.5 * xy

    def drag_of(u, v, cu, cv):
        a = cu - u
        b = cv - v
        y = a * a + b * b + 0.01
        return y * lax.rsqrt(y)

    def velocity_step(k):
        last = k == ITERS - 1
        total = jnp.zeros((DEEP, C), f32)
        for p, n in chunks if last else everywhere:
            lane = lax.broadcasted_iota(jnp.int32, (n, C), 1)
            rows = pl.ds(p, n)
            dxx = shifted(sig[0, 0, rows], sig[0, 1, rows], lane)
            dxy = shifted(sig[2, 0, rows], sig[2, 1, rows], lane)
            spin = cor[rows]
            for w in range(1 if last else 2):
                src = edge_force if w else force
                hi, lo = pl.ds(p + 1, n), pl.ds(p - 1, n)
                east = dxx[w] + (sig[2, w, hi] - sig[2, w, lo])
                north = dxy[w] + (sig[1, w, hi] - sig[1, w, lo])
                u, v = vel[0, w, rows], vel[1, w, rows]
                cu, cv = src[2, rows], src[3, rows]
                im = inv_mass[w, rows]
                if k == 0:
                    bu = u + src[0, rows] * im
                    bv = v + src[1, rows] * im
                    base[0, w, rows] = bu
                    base[1, w, rows] = bv
                else:
                    bu, bv = base[0, w, rows], base[1, w, rows]
                grip = drag_of(u, v, cu, cv) * im
                scale = ice[w, rows] / (5.0 + grip)
                push = 0.25 * im
                new_u = (4.0 * u + bu + east * push + grip * cu + spin * v) * scale
                new_v = (4.0 * v + bv + north * push + grip * cv - spin * u) * scale
                if last:
                    vel_out[0, p - PAD : p - PAD + n] = new_u
                    vel_out[1, p - PAD : p - PAD + n] = new_v
                    drag = drag_of(new_u, new_v, cu, cv) * ice[w, rows]
                    ocean[0, p - PAD : p - PAD + n] = drag * (new_u - cu)
                    ocean[1, p - PAD : p - PAD + n] = drag * (new_v - cv)
                else:
                    vel[0, w, rows] = new_u
                    vel[1, w, rows] = new_v
                if w == 0 and PAD <= p < T:
                    du = new_u - u
                    dv = new_v - v
                    square = du * du + dv * dv
                    for g in range(0, n, DEEP):
                        total = total + square[g : g + DEEP]
        sums[k : k + 1] = jnp.sum(total, axis=0, keepdims=True)

    stress_step(False)

    share = pl.ds(0, 4 * B + 2 * DEEP)

    def forward(to_north):
        band = jnp.where(to_north, G - 1, 0)

        @pl.when(band != gx)
        def _():
            settle(cor.at[share], f_recv.at[band])

        src = pl.ds(pl.multiple_of(jnp.where(to_north, T - DEEP, PAD), DEEP), DEEP)
        dst = pl.ds(pl.multiple_of(jnp.where(to_north, PAD - DEEP, T), DEEP), DEEP)
        step = jnp.where(to_north, 1, Y - 1)
        way = to_north.astype(jnp.int32)

        @pl.when(jnp.where(to_north, gy < Y - 1, gy > 0))
        def _():
            remote(force.at[:, src], force.at[:, dst], p_send.at[way], p_recv.at[way], at(0, step)).start()
            remote(
                f_in.at[band + 1], f_in.at[jnp.where(to_north, 0, G + 1)], p_send.at[way], p_recv.at[way], at(0, step)
            ).start()

    forward(low_half)
    forward(jnp.logical_not(low_half))
    for b in range(1, G - 1):

        @pl.when(gx != b)
        def _():
            settle(cor.at[share], f_recv.at[b])

    skirt = pl.ds(0, 4 * DEEP + 2 * DEEP)

    @pl.when(has_south)
    def _():
        settle(cor.at[pack8], y_send.at[0])
        settle(cor.at[skirt], p_recv.at[1])

    @pl.when(has_north)
    def _():
        settle(cor.at[pack8], y_send.at[1])
        settle(cor.at[skirt], p_recv.at[0])

    for s in range(0, G + 2, 8):
        t = f_in[s : s + 8].reshape(8 * 2 * DEEP, LANES).T
        for b in range(s, min(s + 8, G + 2)):
            turn = LANES - (2 * DEEP * (b - s) + DEEP)
            for c in range(4):
                part = t[c * B : (c + 1) * B]
                if b == 0:
                    edge_force[c, under] = pltpu.roll(part[B - DEEP :], turn, 1)
                elif b == G + 1:
                    edge_force[c, over] = pltpu.roll(part[:DEEP], turn, 1)
                else:
                    edge_force[c, PAD + (b - 1) * B : PAD + b * B] = pltpu.roll(part, turn, 1)

    sums[...] = jnp.zeros_like(sums)
    velocity_step(0)
    for k in range(1, ITERS):
        stress_step(k == ITERS - 1)
        velocity_step(k)

    for j in range(G - 1):
        to = others(j)
        remote(
            ocean.at[:, pl.ds(pl.multiple_of(to * B, B), B)], os_out.at[:, :, own_columns],
            o_sem.at[0], o_sem.at[1], {"gx": to, "gy": gy},
        ).start()
    for d in range(1, Y):
        remote(sums, partial_y.at[gy], r_send.at[0], r_recv.at[0], at(0, d)).start()
    partial_y[gy] = sums[...]
    os_out[:, :, own_columns] = ocean[:, mine]
    settle(partial_y.at[pl.ds(0, Y - 1)], r_recv.at[0])
    partial_x[gx] = jnp.sum(partial_y[...], axis=0)
    for d in range(1, G):
        remote(partial_x.at[gx], partial_x.at[gx], r_send.at[1], r_recv.at[1], at(d, 0)).start()
    most = pl.ds(0, (G - 1) * C)
    settle(os_out.at[:, :, most], o_sem.at[1])
    settle(partial_x.at[pl.ds(0, G - 1)], r_recv.at[1])
    total = jnp.sum(partial_x[...], axis=0)
    lane1 = lax.broadcasted_iota(jnp.int32, (1, LANES), 1)
    answer = jnp.zeros((1, LANES), f32)
    for k in range(ITERS):
        answer = jnp.where(lane1 == k, jnp.sum(total[k : k + 1]), answer)
    res_out[...] = answer[0, :ITERS]
    settle(bands.at[:, :, most], f_send.at[0])
    settle(f_out.at[pl.ds(0, G - 1)], f_send.at[1])
    settle(os_out.at[:, :, most], o_sem.at[0])
    for copy in sides:
        copy.wait_send()

    @pl.when(has_south)
    def _():
        for copy in south:
            copy.wait_send()
        settle(cor.at[skirt], p_send.at[0])

    @pl.when(has_north)
    def _():
        for copy in north:
            copy.wait_send()
        settle(cor.at[skirt], p_send.at[1])

    settle(partial_y.at[pl.ds(0, Y - 1)], r_send.at[0])
    settle(partial_x.at[pl.ds(0, G - 1)], r_send.at[1])


def store(vel, sig, res, ocean, vel_out, sig_out, res_out, ocean_out, sem):
    pairs = ((sig, sig_out), (vel, vel_out), (ocean, ocean_out), (res, res_out))
    copies = [pltpu.make_async_copy(src, dst, sem.at[n]) for n, (src, dst) in enumerate(pairs)]
    for copy in copies:
        copy.start()
    for copy in copies:
        copy.wait()


def local(velocity, stress, ice_mass, strength, land_mask, ocean_forcing):
    G, Y = lax.axis_size("gx"), lax.axis_size("gy")
    R, C = velocity.shape[1:]
    B = ocean_forcing.shape[1]
    f32 = jnp.float32
    rows = R + 2 * PAD
    slots = (G + 2 + 7) // 8 * 8
    dma = pltpu.SemaphoreType.DMA
    any_space = pl.BlockSpec(memory_space=pl.ANY)
    vmem_space = pl.BlockSpec(memory_space=pltpu.VMEM)
    done = pl.pallas_call(
        functools.partial(kernel, G, Y, R, C, B),
        out_shape=(
            pltpu.VMEM(velocity.shape, f32),
            pltpu.VMEM(stress.shape, f32),
            pltpu.VMEM((ITERS,), f32),
            pltpu.VMEM((2,) + ocean_forcing.shape[1:], f32),
        ),
        in_specs=[any_space] * 6,
        out_specs=(vmem_space,) * 4,
        scratch_shapes=[
            pltpu.VMEM((2, 2, rows, C), f32),
            pltpu.VMEM((3, 2, rows, C), f32),
            pltpu.VMEM((3, rows, C), f32),
            pltpu.VMEM((rows, C), f32),
            pltpu.VMEM((rows, C), f32),
            pltpu.VMEM((rows, C), jnp.int32),
            pltpu.VMEM((2, rows, C), f32),
            pltpu.VMEM((2, rows, C), f32),
            pltpu.VMEM((2, rows, C), f32),
            pltpu.VMEM((2, 2, rows, C), f32),
            pltpu.VMEM((4, rows, C), f32),
            pltpu.VMEM((4, rows, C), f32),
            pltpu.VMEM((rows, C), f32),
            pltpu.VMEM(ocean_forcing.shape, f32),
            pltpu.VMEM((2, R, C), f32),
            pltpu.VMEM((8, DEEP, R), f32),
            pltpu.VMEM((8, DEEP, R), f32),
            pltpu.VMEM((2, DEEP, LANES), f32),
            pltpu.VMEM((4, DEEP, LANES), f32),
            pltpu.VMEM((8, 2 * DEEP, R + 2 * LANES), f32),
            pltpu.VMEM((G, 2 * DEEP, LANES), f32),
            pltpu.VMEM((slots, 2 * DEEP, LANES), f32),
            pltpu.VMEM((DEEP, LANES), f32),
            pltpu.VMEM((Y, DEEP, LANES), f32),
            pltpu.VMEM((G, DEEP, LANES), f32),
            dma((6,)),
            dma((2,)),
            dma((G,)),
            dma((6,)),
            dma((6,)),
            dma((2,)),
            dma((2,)),
            dma((2,)),
            dma((2,)),
            dma((2,)),
            dma((2,)),
            dma((2,)),
        ],
        compiler_params=pltpu.CompilerParams(collective_id=0, has_side_effects=True),
    )(velocity, stress, ice_mass, strength, land_mask, ocean_forcing)
    return pl.pallas_call(
        store,
        out_shape=tuple(jax.ShapeDtypeStruct(x.shape, f32) for x in done),
        in_specs=[vmem_space] * 4,
        out_specs=(any_space,) * 4,
        scratch_shapes=[dma((4,))],
    )(*[pltpu.with_memory_space_constraint(x, pltpu.VMEM) for x in done])


def solution(mesh):
    placed = (
        P(None, "gy", "gx"),
        P(None, "gy", "gx"),
        P("gy", "gx"),
        P("gy", "gx"),
        P("gy", "gx"),
        P(None, ("gy", "gx"), None),
    )
    return jax.shard_map(
        local,
        mesh=mesh,
        in_specs=placed,
        out_specs=(P(None, "gy", "gx"), P(None, "gy", "gx"), P(), P(None, ("gy", "gx"), None)),
        check_vma=False,
    )
```

profile of v0, /device:TPU:0, one launch (start us, length us, event | category | flops | bytes accessed | tf_op | source)
XLA Modules:
  0.0 33.6 jit_solution(7657041279920750055)
XLA Ops:
  0.6 32.0 %shard_map.93 = (f32[2,256,128]{2,1,0:T(8,128)S(1)}, f32[3,256,128]{2,1,0:T(8,128)S(1)}, f32[4]{0:T(128)S(1)}, f32[2,32,1024]{2,1,0:T(8,128)S(1)}) custom-call(f32[2,256,128]{2,1,0:T(8,128)} %vel_in.1, f32[3,256,128]{2,1,0:T(8,128)} %sig_in.1, f32[256,128]{1,0:T(8,128)} %mass_in.1, f32[256,128]{1,0:T(8,128)} %strength_in.1, s32[256,128]{1,0:T(8,128)} %mask_in.1, ...), custom_call_target="tpu_custom_call" | custom-call | tf_op jit(solution)/shard_map/pallas_call | solution.py:457
  32.6 1.0 %shard_map.94 = (f32[2,256,128]{2,1,0:T(8,128)}, f32[3,256,128]{2,1,0:T(8,128)}, f32[4]{0:T(128)}, f32[2,32,1024]{2,1,0:T(8,128)}) custom-call(f32[2,256,128]{2,1,0:T(8,128)S(1)} %get-tuple-element.8.vel, f32[3,256,128]{2,1,0:T(8,128)S(1)} %get-tuple-element.9.sig, f32[4]{0:T(128)S(1)} %get-tuple-element.10.res, f32[2,32,1024]{2,1,0:T(8,128)S(1)} %get-tuple-element.11.ocean), custom_call_target="tpu_custom_call" | custom-call | tf_op jit(solution)/shard_map/pallas_call | solution.py:508
where the time goes:
time: 33.8 us; the launch traced here: 33.6 us
  Pallas kernels  33 us (98%)
  between operations  0.64 us (2%)
    pallas_call x1, Pallas kernels, local(): pl.pallas_call(functools.partial(kernel, G, Y, R, C, B), out_shape=(pltpu...  32 us
    pallas_call x1, Pallas kernels, local(): pl.pallas_call(store, out_shape=tuple((jax.ShapeDtypeStruct(x.shape, f32)...  0.96 us

commit v1 on v0

--- a/solution.py
+++ b/solution.py
@@ -12,6 +12,7 @@
 PAD = 16
 LANES = 128
 CHUNK = 16
+REACH = 6
 MESH = pl.DeviceIdType.MESH
 SW, SE, NW, NE = range(4)
 
@@ -21,7 +22,7 @@
     vel_in, sig_in, mass_in, strength_in, mask_in, forcing_in,
     vel_out, sig_out, res_out, os_out,
     vel, sig, raw_sig, raw_mass, raw_strength, raw_mask, pull, inv_mass, ice, base, force, edge_force, cor,
-    bands, ocean, low, high, corner_out, corner_in, strip, f_out, f_in, sums, partial_y, partial_x,
+    bands, ocean, low, high, corner_out, corner_in, strip, f_out, f_in, sums, partial,
     in_sem, f_send, f_recv, h_send, h_recv, y_send, y_recv, p_send, p_recv, o_sem, r_send, r_recv,
 ):
     gx = lax.axis_index("gx")
@@ -41,8 +42,7 @@
         pltpu.make_async_copy(ref, ref, sem).wait()
 
     barrier = pltpu.get_barrier_semaphore()
-    partners = [(d, 0) for d in range(1, G)] + [(0, d) for d in range(1, Y)]
-    partners += [(dx, dy) for dx in (-1, 1) for dy in (-1, 1)]
+    partners = [(dx, dy) for dx in range(G) for dy in range(Y) if dx or dy]
     for dx, dy in partners:
         pl.semaphore_signal(barrier, inc=1, device_id=at(dx, dy), device_id_type=MESH)
     inner = pl.ds(PAD, R)
@@ -70,7 +70,7 @@
         raw_mask[rows] = jnp.zeros((DEEP, C), jnp.int32)
         for c in range(4):
             force[c, rows] = jnp.zeros((DEEP, C), f32)
-        f_in[slot] = jnp.zeros((2 * DEEP, LANES), f32)
+        f_in[slot] = jnp.zeros((2 * REACH, LANES), f32)
         for c in corners:
             corner_in[c] = jnp.where(lane8 // (2 * DEEP) == 5, 1.0, 0.0)
 
@@ -88,15 +88,29 @@
         cor[n : n + DEEP] = 0.3 + 1.2 * (lat + 0.5) / (R * Y)
 
     loads[0].wait()
-    for c in range(G):
-        t = bands[:, :, c * C : (c + 1) * C].reshape(4 * B, C).T
-        f_out[(c + 1) % G, 0:DEEP, 0 : 4 * B] = t[C - DEEP : C]
-        f_out[(c + G - 1) % G, DEEP : 2 * DEEP, 0 : 4 * B] = t[0:DEEP]
-    f_in[gx + 1] = f_out[gx]
+    low_half = gx < G // 2
     own_columns = pl.ds(pl.multiple_of(gx * C, C), C)
     mine = pl.ds(pl.multiple_of(gx * B, B), B)
     padded_mine = pl.ds(pl.multiple_of(PAD + gx * B, DEEP), B)
-    force[:, padded_mine] = bands[:, :, own_columns]
+    pl.semaphore_wait(barrier, len(partners))
+    def others(j):
+        down = G - 1 - j
+        down = down - (down <= gx).astype(jnp.int32)
+        return jnp.where(low_half, down, j + (j >= gx).astype(jnp.int32))
+
+    def send_block(j):
+        to = others(j)
+        columns = pl.ds(pl.multiple_of(to * C, C), C)
+        where = {"gx": to, "gy": gy}
+        remote(bands.at[:, :, columns], force.at[:, padded_mine], f_send.at[0], f_recv.at[gx], where).start()
+
+    def send_strip(j):
+        to = others(j)
+        where = {"gx": to, "gy": gy}
+        remote(f_out.at[to], f_in.at[gx + 1], f_send.at[1], f_recv.at[gx], where).start()
+
+    for j in range(2):
+        send_block(j)
     for copy in loads[1:]:
         copy.wait()
     fields = [vel.at[0, 0], vel.at[1, 0], raw_sig.at[0], raw_sig.at[1], raw_sig.at[2], raw_mass, raw_strength, raw_mask]
@@ -119,22 +133,6 @@
     corner_out[0] = west_tile
     corner_out[1] = east_tile
 
-    pl.semaphore_wait(barrier, len(partners))
-    low_half = gx < G // 2
-
-    def others(j):
-        down = G - 1 - j
-        down = down - (down <= gx).astype(jnp.int32)
-        return jnp.where(low_half, down, j + (j >= gx).astype(jnp.int32))
-
-    def forcing_sends(js):
-        for j in js:
-            to = others(j)
-            where = {"gx": to, "gy": gy}
-            columns = pl.ds(pl.multiple_of(to * C, C), C)
-            remote(bands.at[:, :, columns], force.at[:, padded_mine], f_send.at[0], f_recv.at[gx], where).start()
-            remote(f_out.at[to], f_in.at[gx + 1], f_send.at[1], f_recv.at[gx], where).start()
-
     near, far = pl.ds(0, DEEP), pl.ds(DEEP, DEEP)
     centre = pl.ds(LANES, R)
     bottom, top = pl.ds(PAD, DEEP), pl.ds(T - DEEP, DEEP)
@@ -145,7 +143,6 @@
             return ref.at[:, 0, rows]
         return ref.at[:, rows] if len(ref.shape) == 3 else ref.at[rows]
 
-    forcing_sends(range(2))
     sides = [
         remote(low, strip.at[:, far, centre], h_send.at[0], h_recv.at[0], at(-1, 0)),
         remote(high, strip.at[:, near, centre], h_send.at[1], h_recv.at[1], at(1, 0)),
@@ -175,7 +172,17 @@
         for ref in stacks:
             remote(rows_of(ref, top), rows_of(ref, under), y_send.at[1], y_recv.at[1], at(0, 1)).start()
 
-    forcing_sends(range(2, G - 1))
+    for c in range(G):
+        t = bands[:, :, c * C : (c + 1) * C].reshape(4 * B, C).T
+        f_out[(c + 1) % G, 0:REACH, 0 : 4 * B] = t[C - REACH : C]
+        f_out[(c + G - 1) % G, REACH : 2 * REACH, 0 : 4 * B] = t[0:REACH]
+    for j in range(2):
+        send_strip(j)
+    for j in range(2, G - 1):
+        send_block(j)
+        send_strip(j)
+    f_in[gx + 1] = f_out[gx]
+    force[:, padded_mine] = bands[:, :, own_columns]
 
     chunks = [(n, CHUNK) for n in range(PAD, T, CHUNK)]
     skirts = [(PAD - DEEP, DEEP), (T, DEEP)]
@@ -246,9 +253,10 @@
         )
 
     everywhere = skirts[:1] + chunks + skirts[1:]
-
-    def stress_step(last):
-        for p, n in everywhere:
+    row8 = lax.broadcasted_iota(jnp.int32, (DEEP, C), 0)
+
+    def stress_step(last, spans, merge=False):
+        for p, n, keep in spans:
             lane = lax.broadcasted_iota(jnp.int32, (n, C), 1)
             rows = pl.ds(p, n)
             dxu = shifted(vel[0, 0, rows], vel[0, 1, rows], lane)
@@ -265,16 +273,20 @@
                 quarter = 0.25 * scaled
                 spread = scaled * div - hold
                 twist = quarter * ten
-                xx = 0.75 * sig[0, w, rows] + (spread + twist)
-                yy = 0.75 * sig[1, w, rows] + (spread - twist)
-                xy = 0.75 * sig[2, w, rows] + quarter * shear
-                sig[0, w, rows] = xx
-                sig[1, w, rows] = yy
-                sig[2, w, rows] = xy
-                if last and w == 0 and PAD <= p < T:
-                    sig_out[0, p - PAD : p - PAD + n] = 0.5 * (xx + yy)
-                    sig_out[1, p - PAD : p - PAD + n] = 0.5 * (xx - yy)
-                    sig_out[2, p - PAD : p - PAD + n] = 0.5 * xy
+                old = [sig[c, w, rows] for c in range(3)]
+                new = [
+                    0.75 * old[0] + (spread + twist),
+                    0.75 * old[1] + (spread - twist),
+                    0.75 * old[2] + quarter * shear,
+                ]
+                if keep is not None:
+                    new = [jnp.where(keep, a, b) for a, b in zip(new, old)]
+                for c in range(3):
+                    sig[c, w, rows] = new[c]
+                if last and w == 0 and PAD <= p < T and (keep is None or merge):
+                    sig_out[0, p - PAD : p - PAD + n] = 0.5 * (new[0] + new[1])
+                    sig_out[1, p - PAD : p - PAD + n] = 0.5 * (new[0] - new[1])
+                    sig_out[2, p - PAD : p - PAD + n] = 0.5 * new[2]
 
     def drag_of(u, v, cu, cv):
         a = cu - u
@@ -282,10 +294,12 @@
         y = a * a + b * b + 0.01
         return y * lax.rsqrt(y)
 
-    def velocity_step(k):
+    def velocity_step(k, spans, total, merge=False):
         last = k == ITERS - 1
-        total = jnp.zeros((DEEP, C), f32)
-        for p, n in chunks if last else everywhere:
+        for p, n, keep in spans:
+            inside = PAD <= p < T
+            if last and not inside:
+                continue
             lane = lax.broadcasted_iota(jnp.int32, (n, C), 1)
             rows = pl.ds(p, n)
             dxx = shifted(sig[0, 0, rows], sig[0, 1, rows], lane)
@@ -311,7 +325,10 @@
                 push = 0.25 * im
                 new_u = (4.0 * u + bu + east * push + grip * cu + spin * v) * scale
                 new_v = (4.0 * v + bv + north * push + grip * cv - spin * u) * scale
-                if last:
+                if keep is not None:
+                    new_u = jnp.where(keep, new_u, u)
+                    new_v = jnp.where(keep, new_v, v)
+                if last and (keep is None or merge):
                     vel_out[0, p - PAD : p - PAD + n] = new_u
                     vel_out[1, p - PAD : p - PAD + n] = new_v
                     drag = drag_of(new_u, new_v, cu, cv) * ice[w, rows]
@@ -320,17 +337,20 @@
                 else:
                     vel[0, w, rows] = new_u
                     vel[1, w, rows] = new_v
-                if w == 0 and PAD <= p < T:
+                if w == 0 and inside:
                     du = new_u - u
                     dv = new_v - v
                     square = du * du + dv * dv
                     for g in range(0, n, DEEP):
                         total = total + square[g : g + DEEP]
-        sums[k : k + 1] = jnp.sum(total, axis=0, keepdims=True)
-
-    stress_step(False)
-
-    share = pl.ds(0, 4 * B + 2 * DEEP)
+        return total
+
+    def spans_of(lo, hi):
+        return [(p, min(CHUNK, hi - p), None) for p in range(lo, hi, CHUNK)]
+
+    stress_step(False, [(p, n, None) for p, n in everywhere])
+
+    share = pl.ds(0, 4 * B + 2 * REACH)
 
     def forward(to_north):
         band = jnp.where(to_north, G - 1, 0)
@@ -353,66 +373,119 @@
 
     forward(low_half)
     forward(jnp.logical_not(low_half))
-    for b in range(1, G - 1):
-
+    skirt = pl.ds(0, 4 * DEEP + 2 * REACH)
+
+    def arrive(bs):
+        for b in bs:
+
+            @pl.when(gx != b)
+            def _():
+                settle(cor.at[share], f_recv.at[b])
+
+    def edges(bs):
+        for s in range(0, len(bs), 8):
+            group = bs[s : s + 8]
+            parts = [f_in[b + 1] for b in group]
+            fill = LANES - 2 * REACH * len(group)
+            t = jnp.concatenate(parts + [jnp.zeros((fill, LANES), f32)], axis=0).T
+            for n, b in enumerate(group):
+                turn = LANES - (2 * REACH * n + REACH)
+                for c in range(4):
+                    part = t[c * B : (c + 1) * B]
+                    if b == -1:
+                        edge_force[c, under] = pltpu.roll(part[B - DEEP :], turn, 1)
+                    elif b == G:
+                        edge_force[c, over] = pltpu.roll(part[:DEEP], turn, 1)
+                    else:
+                        edge_force[c, PAD + b * B : PAD + (b + 1) * B] = pltpu.roll(part, turn, 1)
+
+    def send_rows(b, r, n):
         @pl.when(gx != b)
         def _():
-            settle(cor.at[share], f_recv.at[b])
-
-    skirt = pl.ds(0, 4 * DEEP + 2 * DEEP)
-
-    @pl.when(has_south)
-    def _():
-        settle(cor.at[pack8], y_send.at[0])
-        settle(cor.at[skirt], p_recv.at[1])
-
-    @pl.when(has_north)
-    def _():
-        settle(cor.at[pack8], y_send.at[1])
-        settle(cor.at[skirt], p_recv.at[0])
-
-    for s in range(0, G + 2, 8):
-        t = f_in[s : s + 8].reshape(8 * 2 * DEEP, LANES).T
-        for b in range(s, min(s + 8, G + 2)):
-            turn = LANES - (2 * DEEP * (b - s) + DEEP)
-            for c in range(4):
-                part = t[c * B : (c + 1) * B]
-                if b == 0:
-                    edge_force[c, under] = pltpu.roll(part[B - DEEP :], turn, 1)
-                elif b == G + 1:
-                    edge_force[c, over] = pltpu.roll(part[:DEEP], turn, 1)
-                else:
-                    edge_force[c, PAD + (b - 1) * B : PAD + b * B] = pltpu.roll(part, turn, 1)
-
-    sums[...] = jnp.zeros_like(sums)
-    velocity_step(0)
-    for k in range(1, ITERS):
-        stress_step(k == ITERS - 1)
-        velocity_step(k)
-
-    for j in range(G - 1):
-        to = others(j)
-        remote(
-            ocean.at[:, pl.ds(pl.multiple_of(to * B, B), B)], os_out.at[:, :, own_columns],
-            o_sem.at[0], o_sem.at[1], {"gx": to, "gy": gy},
-        ).start()
-    for d in range(1, Y):
-        remote(sums, partial_y.at[gy], r_send.at[0], r_recv.at[0], at(0, d)).start()
-    partial_y[gy] = sums[...]
+            remote(
+                ocean.at[:, pl.ds(b * B + r, n)], os_out.at[:, pl.ds(r, n), own_columns],
+                o_sem.at[0], o_sem.at[1], {"gx": b, "gy": gy},
+            ).start()
+
+    def phases(is_low):
+        late = list(range(G // 2, G // 2 + G // 4)) if is_low else list(range(G // 2 - G // 4, G // 2))
+        early = [b for b in range(G) if b not in late]
+        w0, w1 = PAD + late[0] * B, PAD + (late[-1] + 1) * B
+        arrive([b for b in early if 0 < b < G - 1])
+
+        @pl.when(has_south)
+        def _():
+            settle(cor.at[pack8], y_send.at[0])
+            settle(cor.at[skirt], p_recv.at[1])
+
+        @pl.when(has_north)
+        def _():
+            settle(cor.at[pack8], y_send.at[1])
+            settle(cor.at[skirt], p_recv.at[0])
+
+        edges([-1] + early + [G])
+        outer = (
+            [(PAD - DEEP, DEEP, None)] + spans_of(PAD, w0 - DEEP) + spans_of(w1 + DEEP, T) + [(T, DEEP, None)]
+        )
+        rims = ((w0 - DEEP, DEEP), (w1, DEEP))
+
+        def first(h):
+            if h == 0:
+                return outer + [(p, n, None) for p, n in rims]
+            return outer + [(*rims[0], row8 < DEEP - h), (*rims[1], row8 >= h)]
+
+        def second(h):
+            inside = spans_of(w0, w1)
+            if h == 0:
+                return inside
+            return inside + [(*rims[0], row8 >= DEEP - h), (*rims[1], row8 < h)]
+
+        totals = [jnp.zeros((DEEP, C), f32)] * ITERS
+        totals[0] = velocity_step(0, first(0), totals[0])
+        for k in range(1, ITERS):
+            stress_step(k == ITERS - 1, first(2 * k - 1))
+            totals[k] = velocity_step(k, first(2 * k), totals[k])
+        order = list(range(G - 1, -1, -1)) if is_low else list(range(G))
+        rest = []
+        for b in order:
+            if b in late:
+                rest.append((b, 0, B))
+                continue
+            r, n = 0, B
+            if b == late[0] - 1:
+                n -= DEEP
+                rest.append((b, n, DEEP))
+            elif b == late[-1] + 1:
+                r, n = DEEP, n - DEEP
+                rest.append((b, 0, DEEP))
+            if n:
+                send_rows(b, r, n)
+        arrive(late)
+        edges(late)
+        totals[0] = velocity_step(0, second(0), totals[0])
+        for k in range(1, ITERS):
+            stress_step(k == ITERS - 1, second(2 * k - 1), True)
+            totals[k] = velocity_step(k, second(2 * k), totals[k], True)
+        answer = jnp.zeros((1, LANES), f32)
+        for k in range(ITERS):
+            answer = jnp.where(lane1 == k, jnp.sum(totals[k]), answer)
+        sums[...] = answer
+        me = gx * Y + gy
+        for dx, dy in partners:
+            remote(sums, partial.at[me], r_send.at[0], r_recv.at[0], at(dx, dy)).start()
+        partial[me] = answer
+        for b, r, n in rest:
+            send_rows(b, r, n)
+
+    lane1 = lax.broadcasted_iota(jnp.int32, (1, LANES), 1)
+    pl.when(low_half)(lambda: phases(True))
+    pl.when(jnp.logical_not(low_half))(lambda: phases(False))
     os_out[:, :, own_columns] = ocean[:, mine]
-    settle(partial_y.at[pl.ds(0, Y - 1)], r_recv.at[0])
-    partial_x[gx] = jnp.sum(partial_y[...], axis=0)
-    for d in range(1, G):
-        remote(partial_x.at[gx], partial_x.at[gx], r_send.at[1], r_recv.at[1], at(d, 0)).start()
     most = pl.ds(0, (G - 1) * C)
     settle(os_out.at[:, :, most], o_sem.at[1])
-    settle(partial_x.at[pl.ds(0, G - 1)], r_recv.at[1])
-    total = jnp.sum(partial_x[...], axis=0)
-    lane1 = lax.broadcasted_iota(jnp.int32, (1, LANES), 1)
-    answer = jnp.zeros((1, LANES), f32)
-    for k in range(ITERS):
-        answer = jnp.where(lane1 == k, jnp.sum(total[k : k + 1]), answer)
-    res_out[...] = answer[0, :ITERS]
+    peers = pl.ds(0, len(partners))
+    settle(partial.at[peers], r_recv.at[0])
+    res_out[...] = jnp.sum(partial[...], axis=0)[0, :ITERS]
     settle(bands.at[:, :, most], f_send.at[0])
     settle(f_out.at[pl.ds(0, G - 1)], f_send.at[1])
     settle(os_out.at[:, :, most], o_sem.at[0])
@@ -431,8 +504,7 @@
             copy.wait_send()
         settle(cor.at[skirt], p_send.at[1])
 
-    settle(partial_y.at[pl.ds(0, Y - 1)], r_send.at[0])
-    settle(partial_x.at[pl.ds(0, G - 1)], r_send.at[1])
+    settle(partial.at[peers], r_send.at[0])
 
 
 def store(vel, sig, res, ocean, vel_out, sig_out, res_out, ocean_out, sem):
@@ -450,7 +522,6 @@
     B = ocean_forcing.shape[1]
     f32 = jnp.float32
     rows = R + 2 * PAD
-    slots = (G + 2 + 7) // 8 * 8
     dma = pltpu.SemaphoreType.DMA
     any_space = pl.BlockSpec(memory_space=pl.ANY)
     vmem_space = pl.BlockSpec(memory_space=pltpu.VMEM)
@@ -485,11 +556,10 @@
             pltpu.VMEM((2, DEEP, LANES), f32),
             pltpu.VMEM((4, DEEP, LANES), f32),
             pltpu.VMEM((8, 2 * DEEP, R + 2 * LANES), f32),
-            pltpu.VMEM((G, 2 * DEEP, LANES), f32),
-            pltpu.VMEM((slots, 2 * DEEP, LANES), f32),
-            pltpu.VMEM((DEEP, LANES), f32),
-            pltpu.VMEM((Y, DEEP, LANES), f32),
-            pltpu.VMEM((G, DEEP, LANES), f32),
+            pltpu.VMEM((G, 2 * REACH, LANES), f32),
+            pltpu.VMEM((G + 2, 2 * REACH, LANES), f32),
+            pltpu.VMEM((1, LANES), f32),
+            pltpu.VMEM((G * Y, 1, LANES), f32),
             dma((6,)),
             dma((2,)),
             dma((G,)),
@@ -500,8 +570,8 @@
             dma((2,)),
             dma((2,)),
             dma((2,)),
-            dma((2,)),
-            dma((2,)),
+            dma((1,)),
+            dma((1,)),
         ],
         compiler_params=pltpu.CompilerParams(collective_id=0, has_side_effects=True),
     )(velocity, stress, ice_mass, strength, land_mask, ocean_forcing)

time: 33.8 us -> 32.5 us (0.962)
  Pallas kernels: 33 us -> 31.7 us
    pallas_call x1, Pallas kernels: 32 us -> 30.7 us  [local(): pl.pallas_call(functools.partial(kernel, G, Y, R, C, B), out_shape=(pltpu...]
where the time goes in v1:
time: 32.5 us; the launch traced here: 32.3 us
  Pallas kernels  31.7 us (98%)
  between operations  0.64 us (2%)
    pallas_call x1, Pallas kernels, local(): pl.pallas_call(functools.partial(kernel, G, Y, R, C, B), out_shape=(pltpu...  30.7 us
    pallas_call x1, Pallas kernels, local(): pl.pallas_call(store, out_shape=tuple((jax.ShapeDtypeStruct(x.shape, f32)...  0.96 us

profile of v1, /device:TPU:0, one launch (start us, length us, event | category | flops | bytes accessed | tf_op | source)
XLA Modules:
  0.0 32.3 jit_solution(5401537193199544072)
XLA Ops:
  0.6 30.7 %shard_map.93 = (f32[2,256,128]{2,1,0:T(8,128)S(1)}, f32[3,256,128]{2,1,0:T(8,128)S(1)}, f32[4]{0:T(128)S(1)}, f32[2,32,1024]{2,1,0:T(8,128)S(1)}) custom-call(f32[2,256,128]{2,1,0:T(8,128)} %vel_in.1, f32[3,256,128]{2,1,0:T(8,128)} %sig_in.1, f32[256,128]{1,0:T(8,128)} %mass_in.1, f32[256,128]{1,0:T(8,128)} %strength_in.1, s32[256,128]{1,0:T(8,128)} %mask_in.1, ...), custom_call_target="tpu_custom_call" | custom-call | tf_op jit(solution)/shard_map/pallas_call | solution.py:528
  31.4 1.0 %shard_map.94 = (f32[2,256,128]{2,1,0:T(8,128)}, f32[3,256,128]{2,1,0:T(8,128)}, f32[4]{0:T(128)}, f32[2,32,1024]{2,1,0:T(8,128)}) custom-call(f32[2,256,128]{2,1,0:T(8,128)S(1)} %get-tuple-element.8.vel, f32[3,256,128]{2,1,0:T(8,128)S(1)} %get-tuple-element.9.sig, f32[4]{0:T(128)S(1)} %get-tuple-element.10.res, f32[2,32,1024]{2,1,0:T(8,128)S(1)} %get-tuple-element.11.ocean), custom_call_target="tpu_custom_call" | custom-call | tf_op jit(solution)/shard_map/pallas_call | solution.py:578

commit v2 on v1

--- a/solution.py
+++ b/solution.py
@@ -23,7 +23,7 @@
     vel_out, sig_out, res_out, os_out,
     vel, sig, raw_sig, raw_mass, raw_strength, raw_mask, pull, inv_mass, ice, base, force, edge_force, cor,
     bands, ocean, low, high, corner_out, corner_in, strip, f_out, f_in, sums, partial,
-    in_sem, f_send, f_recv, h_send, h_recv, y_send, y_recv, p_send, p_recv, o_sem, r_send, r_recv,
+    in_sem, f_send, f_recv, h_send, h_recv, y_send, y_recv, p_send, p_recv, o_sem, r_send, r_recv, ready,
 ):
     gx = lax.axis_index("gx")
     gy = lax.axis_index("gy")
@@ -43,8 +43,29 @@
 
     barrier = pltpu.get_barrier_semaphore()
     partners = [(dx, dy) for dx in range(G) for dy in range(Y) if dx or dy]
-    for dx, dy in partners:
-        pl.semaphore_signal(barrier, inc=1, device_id=at(dx, dy), device_id_type=MESH)
+    hop = G // 4
+    rounds = 5
+    known = Y - 1
+    for n in range(1, hop + 1):
+        known = known + (gx >= n).astype(jnp.int32) + (gx + n < G).astype(jnp.int32)
+
+    def greet(sem):
+        for n in range(1, hop + 1):
+            for d, there in ((-n, gx >= n), (n, gx + n < G)):
+
+                @pl.when(there)
+                def _():
+                    pl.semaphore_signal(sem, inc=1, device_id={"gx": gx + d, "gy": gy}, device_id_type=MESH)
+
+        for d in range(1, Y):
+            pl.semaphore_signal(sem, inc=1, device_id=at(0, d), device_id_type=MESH)
+
+    def meet(n):
+        pl.semaphore_wait(ready.at[n - 2], known)
+        if n < rounds:
+            greet(ready.at[n - 1])
+
+    greet(barrier)
     inner = pl.ds(PAD, R)
     loads = [
         pltpu.make_async_copy(forcing_in, bands, in_sem.at[0]),
@@ -87,30 +108,49 @@
         lat = (gy * R + (n - PAD) + lax.broadcasted_iota(jnp.int32, (DEEP, C), 0)).astype(f32)
         cor[n : n + DEEP] = 0.3 + 1.2 * (lat + 0.5) / (R * Y)
 
-    loads[0].wait()
     low_half = gx < G // 2
     own_columns = pl.ds(pl.multiple_of(gx * C, C), C)
     mine = pl.ds(pl.multiple_of(gx * B, B), B)
     padded_mine = pl.ds(pl.multiple_of(PAD + gx * B, DEEP), B)
-    pl.semaphore_wait(barrier, len(partners))
-    def others(j):
-        down = G - 1 - j
-        down = down - (down <= gx).astype(jnp.int32)
-        return jnp.where(low_half, down, j + (j >= gx).astype(jnp.int32))
-
-    def send_block(j):
-        to = others(j)
+    pl.semaphore_wait(barrier, known)
+    greet(ready.at[0])
+    loads[0].wait()
+    def to_both(d, send):
+        for to, there in ((gx - d, gx >= d), (gx + d, gx + d < G)):
+            pl.when(there)(lambda: send(to))
+
+    def send_block(to):
         columns = pl.ds(pl.multiple_of(to * C, C), C)
         where = {"gx": to, "gy": gy}
         remote(bands.at[:, :, columns], force.at[:, padded_mine], f_send.at[0], f_recv.at[gx], where).start()
 
-    def send_strip(j):
-        to = others(j)
+    def send_strip(to):
         where = {"gx": to, "gy": gy}
         remote(f_out.at[to], f_in.at[gx + 1], f_send.at[1], f_recv.at[gx], where).start()
 
-    for j in range(2):
-        send_block(j)
+    def send_both(to):
+        send_block(to)
+        send_strip(to)
+
+    to_both(hop, send_block)
+    chunks = [(n, CHUNK) for n in range(PAD, T, CHUNK)]
+    skirts = [(PAD - DEEP, DEEP), (T, DEEP)]
+
+    def prepare(w, p, n, s0, s1, s2, mass, strength, mask):
+        ice[w, p : p + n] = mask
+        pull[w, p : p + n] = 0.25 * strength * mask
+        inv_mass[w, p : p + n] = 1.0 / mass
+        sig[0, w, p : p + n] = (s0 + s1) * mask
+        sig[1, w, p : p + n] = (s0 - s1) * mask
+        sig[2, w, p : p + n] = 2.0 * s2 * mask
+
+    def prepare_main(p, n):
+        rows = pl.ds(p, n)
+        prepare(
+            0, p, n, raw_sig[0, rows], raw_sig[1, rows], raw_sig[2, rows],
+            raw_mass[rows], raw_strength[rows], raw_mask[rows].astype(f32),
+        )
+
     for copy in loads[1:]:
         copy.wait()
     fields = [vel.at[0, 0], vel.at[1, 0], raw_sig.at[0], raw_sig.at[1], raw_sig.at[2], raw_mass, raw_strength, raw_mask]
@@ -155,55 +195,49 @@
         remote(corner_out.at[0], corner_in.at[SE], h_send.at[4], h_recv.at[4], at(-1, 1)),
         remote(corner_out.at[1], corner_in.at[SW], h_send.at[5], h_recv.at[5], at(1, 1)),
     ]
-    for copy in sides:
-        copy.start()
-
-    @pl.when(has_south)
-    def _():
-        for copy in south:
-            copy.start()
-        for ref in stacks:
-            remote(rows_of(ref, bottom), rows_of(ref, over), y_send.at[0], y_recv.at[0], at(0, -1)).start()
-
-    @pl.when(has_north)
-    def _():
-        for copy in north:
-            copy.start()
-        for ref in stacks:
-            remote(rows_of(ref, top), rows_of(ref, under), y_send.at[1], y_recv.at[1], at(0, 1)).start()
-
     for c in range(G):
         t = bands[:, :, c * C : (c + 1) * C].reshape(4 * B, C).T
         f_out[(c + 1) % G, 0:REACH, 0 : 4 * B] = t[C - REACH : C]
         f_out[(c + G - 1) % G, REACH : 2 * REACH, 0 : 4 * B] = t[0:REACH]
-    for j in range(2):
-        send_strip(j)
-    for j in range(2, G - 1):
-        send_block(j)
-        send_strip(j)
+    wraps = ((gx == 0, 0), (gx == G - 1, 1))
+
+    def corners(wrapped):
+        for valid, copies in ((has_south, south), (has_north, north)):
+            for edge, n in wraps:
+                there = edge if wrapped else jnp.logical_not(edge)
+                pl.when(jnp.logical_and(valid, there))(copies[n].start)
+
+    for edge, side in wraps:
+        pl.when(jnp.logical_not(edge))(sides[side].start)
+
+    @pl.when(has_south)
+    def _():
+        for ref in stacks:
+            remote(rows_of(ref, bottom), rows_of(ref, over), y_send.at[0], y_recv.at[0], at(0, -1)).start()
+
+    @pl.when(has_north)
+    def _():
+        for ref in stacks:
+            remote(rows_of(ref, top), rows_of(ref, under), y_send.at[1], y_recv.at[1], at(0, 1)).start()
+
+    to_both(hop, send_strip)
+    meet(2)
+    corners(False)
+    to_both(2 * hop, send_both)
     f_in[gx + 1] = f_out[gx]
     force[:, padded_mine] = bands[:, :, own_columns]
-
-    chunks = [(n, CHUNK) for n in range(PAD, T, CHUNK)]
-    skirts = [(PAD - DEEP, DEEP), (T, DEEP)]
-
-    def prepare(w, p, n, s0, s1, s2, mass, strength, mask):
-        ice[w, p : p + n] = mask
-        pull[w, p : p + n] = 0.25 * strength * mask
-        inv_mass[w, p : p + n] = 1.0 / mass
-        sig[0, w, p : p + n] = (s0 + s1) * mask
-        sig[1, w, p : p + n] = (s0 - s1) * mask
-        sig[2, w, p : p + n] = 2.0 * s2 * mask
-
-    def prepare_main(p, n):
-        rows = pl.ds(p, n)
-        prepare(
-            0, p, n, raw_sig[0, rows], raw_sig[1, rows], raw_sig[2, rows],
-            raw_mass[rows], raw_strength[rows], raw_mask[rows].astype(f32),
-        )
-
-    for p, n in chunks:
-        prepare_main(p, n)
+    meet(3)
+    to_both(3 * hop, send_both)
+    for p, m in chunks:
+        prepare_main(p, m)
+    meet(4)
+    for edge, side in wraps:
+        pl.when(edge)(sides[side].start)
+    meet(5)
+    corners(True)
+    for d in range(G - 1, 0, -1):
+        if d % hop:
+            to_both(d, send_both)
     pack8 = pl.ds(0, 8 * DEEP)
 
     @pl.when(has_north)
@@ -572,6 +606,7 @@
             dma((2,)),
             dma((1,)),
             dma((1,)),
+            pltpu.SemaphoreType.REGULAR((4,)),
         ],
         compiler_params=pltpu.CompilerParams(collective_id=0, has_side_effects=True),
     )(velocity, stress, ice_mass, strength, land_mask, ocean_forcing)

time: 32.5 us -> 30.8 us (0.948)
  Pallas kernels: 31.7 us -> 30 us
    pallas_call x1, Pallas kernels: 30.7 us -> 29 us  [local(): pl.pallas_call(functools.partial(kernel, G, Y, R, C, B), out_shape=(pltpu...]
where the time goes in v2:
time: 30.8 us; the launch traced here: 30.6 us
  Pallas kernels  30 us (97%)
  between operations  0.64 us (2%)
    pallas_call x1, Pallas kernels, local(): pl.pallas_call(functools.partial(kernel, G, Y, R, C, B), out_shape=(pltpu...  29 us
    pallas_call x1, Pallas kernels, local(): pl.pallas_call(store, out_shape=tuple((jax.ShapeDtypeStruct(x.shape, f32)...  0.96 us

profile of v2, /device:TPU:0, one launch (start us, length us, event | category | flops | bytes accessed | tf_op | source)
XLA Modules:
  0.0 30.6 jit_solution(10451836568665372843)
XLA Ops:
  0.6 29.0 %shard_map.93 = (f32[2,256,128]{2,1,0:T(8,128)S(1)}, f32[3,256,128]{2,1,0:T(8,128)S(1)}, f32[4]{0:T(128)S(1)}, f32[2,32,1024]{2,1,0:T(8,128)S(1)}) custom-call(f32[2,256,128]{2,1,0:T(8,128)} %vel_in.1, f32[3,256,128]{2,1,0:T(8,128)} %sig_in.1, f32[256,128]{1,0:T(8,128)} %mass_in.1, f32[256,128]{1,0:T(8,128)} %strength_in.1, s32[256,128]{1,0:T(8,128)} %mask_in.1, ...), custom_call_target="tpu_custom_call" | custom-call | tf_op jit(solution)/shard_map/pallas_call | solution.py:562
  29.7 1.0 %shard_map.94 = (f32[2,256,128]{2,1,0:T(8,128)}, f32[3,256,128]{2,1,0:T(8,128)}, f32[4]{0:T(128)}, f32[2,32,1024]{2,1,0:T(8,128)}) custom-call(f32[2,256,128]{2,1,0:T(8,128)S(1)} %get-tuple-element.8.vel, f32[3,256,128]{2,1,0:T(8,128)S(1)} %get-tuple-element.9.sig, f32[4]{0:T(128)S(1)} %get-tuple-element.10.res, f32[2,32,1024]{2,1,0:T(8,128)S(1)} %get-tuple-element.11.ocean), custom_call_target="tpu_custom_call" | custom-call | tf_op jit(solution)/shard_map/pallas_call | solution.py:613

commit v3 on v2

--- a/solution.py
+++ b/solution.py
@@ -23,7 +23,7 @@
     vel_out, sig_out, res_out, os_out,
     vel, sig, raw_sig, raw_mass, raw_strength, raw_mask, pull, inv_mass, ice, base, force, edge_force, cor,
     bands, ocean, low, high, corner_out, corner_in, strip, f_out, f_in, sums, partial,
-    in_sem, f_send, f_recv, h_send, h_recv, y_send, y_recv, p_send, p_recv, o_sem, r_send, r_recv, ready,
+    in_sem, f_send, f_recv, e_recv, h_send, h_recv, y_send, y_recv, p_send, p_recv, o_sem, r_send, r_recv, ready,
 ):
     gx = lax.axis_index("gx")
     gy = lax.axis_index("gy")
@@ -115,24 +115,59 @@
     pl.semaphore_wait(barrier, known)
     greet(ready.at[0])
     loads[0].wait()
-    def to_both(d, send):
-        for to, there in ((gx - d, gx >= d), (gx + d, gx + d < G)):
+    at_end = jnp.logical_or(gx == 0, gx == G - 1)
+    on_top = (gx == G - 1).astype(jnp.int32)
+    rim_row = on_top * (B - DEEP)
+    rest_row = (1 - on_top) * DEEP
+
+    def to_each(d, send, ways=(-1, 1), only=None):
+        for way in ways:
+            to = gx + way * d
+            there = gx >= d if way < 0 else gx + d < G
+            if only is not None:
+                there = jnp.logical_and(there, only)
             pl.when(there)(lambda: send(to))
 
+    def send_rows_of(to, row, n, sem):
+        columns = pl.ds(pl.multiple_of(to * C, C), C)
+        src = pl.ds(pl.multiple_of(row, DEEP), n)
+        dst = pl.ds(pl.multiple_of(PAD + gx * B + row, DEEP), n)
+        where = {"gx": to, "gy": gy}
+        remote(bands.at[:, src, columns], force.at[:, dst], f_send.at[0], sem, where).start()
+
     def send_block(to):
-        columns = pl.ds(pl.multiple_of(to * C, C), C)
+        pl.when(jnp.logical_not(at_end))(lambda: send_rows_of(to, 0, B, f_recv.at[gx]))
+        if B > DEEP:
+            pl.when(at_end)(lambda: send_rows_of(to, rest_row, B - DEEP, f_recv.at[gx]))
+
+    def strip_to(to, sem):
         where = {"gx": to, "gy": gy}
-        remote(bands.at[:, :, columns], force.at[:, padded_mine], f_send.at[0], f_recv.at[gx], where).start()
+        remote(f_out.at[to], f_in.at[gx + 1], f_send.at[1], sem, where).start()
 
     def send_strip(to):
-        where = {"gx": to, "gy": gy}
-        remote(f_out.at[to], f_in.at[gx + 1], f_send.at[1], f_recv.at[gx], where).start()
+        pl.when(jnp.logical_not(at_end))(lambda: strip_to(to, f_recv.at[gx]))
 
     def send_both(to):
         send_block(to)
         send_strip(to)
 
-    to_both(hop, send_block)
+    def send_rim(to):
+        send_rows_of(to, rim_row, DEEP, e_recv.at[on_top])
+        strip_to(to, e_recv.at[on_top])
+
+    def send_rims(reach):
+        for d in range(max(reach - hop, 0) + 1, min(reach, G - 1) + 1):
+            to_each(d, send_rim, only=at_end)
+
+    def outward(d, send):
+        to_each(d, send, (-1,), low_half)
+        to_each(d, send, (1,), jnp.logical_not(low_half))
+
+    def inward(d, send):
+        to_each(d, send, (1,), low_half)
+        to_each(d, send, (-1,), jnp.logical_not(low_half))
+
+    to_each(hop, send_block)
     chunks = [(n, CHUNK) for n in range(PAD, T, CHUNK)]
     skirts = [(PAD - DEEP, DEEP), (T, DEEP)]
 
@@ -220,24 +255,53 @@
         for ref in stacks:
             remote(rows_of(ref, top), rows_of(ref, under), y_send.at[1], y_recv.at[1], at(0, 1)).start()
 
-    to_both(hop, send_strip)
+    to_each(hop, send_strip)
+    send_rims(hop)
     meet(2)
     corners(False)
-    to_both(2 * hop, send_both)
+    send_rims(2 * hop)
+    for d in range(2 * hop - 1, 0, -1):
+        if d % hop:
+            outward(d, send_both)
+    to_each(2 * hop, send_both)
     f_in[gx + 1] = f_out[gx]
     force[:, padded_mine] = bands[:, :, own_columns]
     meet(3)
-    to_both(3 * hop, send_both)
+    send_rims(3 * hop)
+    to_each(3 * hop, send_both)
     for p, m in chunks:
         prepare_main(p, m)
     meet(4)
+    send_rims(4 * hop)
     for edge, side in wraps:
         pl.when(edge)(sides[side].start)
     meet(5)
     corners(True)
     for d in range(G - 1, 0, -1):
         if d % hop:
-            to_both(d, send_both)
+            inward(d, send_both)
+            if d > 2 * hop:
+                outward(d, send_both)
+    skirt = pl.ds(0, 4 * DEEP + 2 * REACH)
+
+    def forward(to_north):
+        band = G - 1 if to_north else 0
+        way = int(to_north)
+        src = pl.ds(T - DEEP if to_north else PAD, DEEP)
+        dst = pl.ds(PAD - DEEP if to_north else T, DEEP)
+
+        @pl.when(gx != band)
+        def _():
+            settle(cor.at[skirt], e_recv.at[way])
+
+        @pl.when(has_north if to_north else has_south)
+        def _():
+            to = at(0, 1 if to_north else -1)
+            remote(force.at[:, src], force.at[:, dst], p_send.at[way], p_recv.at[way], to).start()
+            remote(f_in.at[band + 1], f_in.at[0 if to_north else G + 1], p_send.at[way], p_recv.at[way], to).start()
+
+    forward(True)
+    forward(False)
     pack8 = pl.ds(0, 8 * DEEP)
 
     @pl.when(has_north)
@@ -385,36 +449,16 @@
     stress_step(False, [(p, n, None) for p, n in everywhere])
 
     share = pl.ds(0, 4 * B + 2 * REACH)
-
-    def forward(to_north):
-        band = jnp.where(to_north, G - 1, 0)
-
-        @pl.when(band != gx)
-        def _():
-            settle(cor.at[share], f_recv.at[band])
-
-        src = pl.ds(pl.multiple_of(jnp.where(to_north, T - DEEP, PAD), DEEP), DEEP)
-        dst = pl.ds(pl.multiple_of(jnp.where(to_north, PAD - DEEP, T), DEEP), DEEP)
-        step = jnp.where(to_north, 1, Y - 1)
-        way = to_north.astype(jnp.int32)
-
-        @pl.when(jnp.where(to_north, gy < Y - 1, gy > 0))
-        def _():
-            remote(force.at[:, src], force.at[:, dst], p_send.at[way], p_recv.at[way], at(0, step)).start()
-            remote(
-                f_in.at[band + 1], f_in.at[jnp.where(to_north, 0, G + 1)], p_send.at[way], p_recv.at[way], at(0, step)
-            ).start()
-
-    forward(low_half)
-    forward(jnp.logical_not(low_half))
-    skirt = pl.ds(0, 4 * DEEP + 2 * REACH)
-
+    rest = pl.ds(0, 4 * (B - DEEP))
     def arrive(bs):
         for b in bs:
 
             @pl.when(gx != b)
             def _():
-                settle(cor.at[share], f_recv.at[b])
+                if 0 < b < G - 1:
+                    settle(cor.at[share], f_recv.at[b])
+                elif B > DEEP:
+                    settle(cor.at[rest], f_recv.at[b])
 
     def edges(bs):
         for s in range(0, len(bs), 8):
@@ -445,7 +489,7 @@
         late = list(range(G // 2, G // 2 + G // 4)) if is_low else list(range(G // 2 - G // 4, G // 2))
         early = [b for b in range(G) if b not in late]
         w0, w1 = PAD + late[0] * B, PAD + (late[-1] + 1) * B
-        arrive([b for b in early if 0 < b < G - 1])
+        arrive(early)
 
         @pl.when(has_south)
         def _():
@@ -480,18 +524,18 @@
             stress_step(k == ITERS - 1, first(2 * k - 1))
             totals[k] = velocity_step(k, first(2 * k), totals[k])
         order = list(range(G - 1, -1, -1)) if is_low else list(range(G))
-        rest = []
+        left = []
         for b in order:
             if b in late:
-                rest.append((b, 0, B))
+                left.append((b, 0, B))
                 continue
             r, n = 0, B
             if b == late[0] - 1:
                 n -= DEEP
-                rest.append((b, n, DEEP))
+                left.append((b, n, DEEP))
             elif b == late[-1] + 1:
                 r, n = DEEP, n - DEEP
-                rest.append((b, 0, DEEP))
+                left.append((b, 0, DEEP))
             if n:
                 send_rows(b, r, n)
         arrive(late)
@@ -508,7 +552,7 @@
         for dx, dy in partners:
             remote(sums, partial.at[me], r_send.at[0], r_recv.at[0], at(dx, dy)).start()
         partial[me] = answer
-        for b, r, n in rest:
+        for b, r, n in left:
             send_rows(b, r, n)
 
     lane1 = lax.broadcasted_iota(jnp.int32, (1, LANES), 1)
@@ -597,6 +641,7 @@
             dma((6,)),
             dma((2,)),
             dma((G,)),
+            dma((2,)),
             dma((6,)),
             dma((6,)),
             dma((2,)),

time: 30.8 us -> 29.1 us (0.945)
  Pallas kernels: 30 us -> 28.4 us
    pallas_call x1, Pallas kernels: 29 us -> 27.4 us  [local(): pl.pallas_call(functools.partial(kernel, G, Y, R, C, B), out_shape=(pltpu...]
where the time goes in v3:
time: 29.1 us; the launch traced here: 29 us
  Pallas kernels  28.4 us (98%)
  between operations  0.64 us (2%)
    pallas_call x1, Pallas kernels, local(): pl.pallas_call(functools.partial(kernel, G, Y, R, C, B), out_shape=(pltpu...  27.4 us
    pallas_call x1, Pallas kernels, local(): pl.pallas_call(store, out_shape=tuple((jax.ShapeDtypeStruct(x.shape, f32)...  0.96 us

profile of v3, /device:TPU:0, one launch (start us, length us, event | category | flops | bytes accessed | tf_op | source)
XLA Modules:
  0.0 29.0 jit_solution(5570569196835592695)
XLA Ops:
  0.6 27.4 %shard_map.93 = (f32[2,256,128]{2,1,0:T(8,128)S(1)}, f32[3,256,128]{2,1,0:T(8,128)S(1)}, f32[4]{0:T(128)S(1)}, f32[2,32,1024]{2,1,0:T(8,128)S(1)}) custom-call(f32[2,256,128]{2,1,0:T(8,128)} %vel_in.1, f32[3,256,128]{2,1,0:T(8,128)} %sig_in.1, f32[256,128]{1,0:T(8,128)} %mass_in.1, f32[256,128]{1,0:T(8,128)} %strength_in.1, s32[256,128]{1,0:T(8,128)} %mask_in.1, ...), custom_call_target="tpu_custom_call" | custom-call | tf_op jit(solution)/shard_map/pallas_call | solution.py:606
  28.0 1.0 %shard_map.94 = (f32[2,256,128]{2,1,0:T(8,128)}, f32[3,256,128]{2,1,0:T(8,128)}, f32[4]{0:T(128)}, f32[2,32,1024]{2,1,0:T(8,128)}) custom-call(f32[2,256,128]{2,1,0:T(8,128)S(1)} %get-tuple-element.8.vel, f32[3,256,128]{2,1,0:T(8,128)S(1)} %get-tuple-element.9.sig, f32[4]{0:T(128)S(1)} %get-tuple-element.10.res, f32[2,32,1024]{2,1,0:T(8,128)S(1)} %get-tuple-element.11.ocean), custom_call_target="tpu_custom_call" | custom-call | tf_op jit(solution)/shard_map/pallas_call | solution.py:658

commit v4 on v3

--- a/solution.py
+++ b/solution.py
@@ -71,9 +71,9 @@
         pltpu.make_async_copy(forcing_in, bands, in_sem.at[0]),
         pltpu.make_async_copy(vel_in, vel.at[:, 0, inner], in_sem.at[1]),
         pltpu.make_async_copy(sig_in, raw_sig.at[:, inner], in_sem.at[2]),
-        pltpu.make_async_copy(mass_in, raw_mass.at[inner], in_sem.at[3]),
-        pltpu.make_async_copy(strength_in, raw_strength.at[inner], in_sem.at[4]),
-        pltpu.make_async_copy(mask_in, raw_mask.at[inner], in_sem.at[5]),
+        pltpu.make_async_copy(mass_in, raw_mass.at[inner], in_sem.at[1]),
+        pltpu.make_async_copy(strength_in, raw_strength.at[inner], in_sem.at[1]),
+        pltpu.make_async_copy(mask_in, raw_mask.at[inner], in_sem.at[2]),
     ]
     for copy in loads:
         copy.start()
@@ -186,8 +186,8 @@
             raw_mass[rows], raw_strength[rows], raw_mask[rows].astype(f32),
         )
 
-    for copy in loads[1:]:
-        copy.wait()
+    settle(bands, in_sem.at[1])
+    settle(bands, in_sem.at[2])
     fields = [vel.at[0, 0], vel.at[1, 0], raw_sig.at[0], raw_sig.at[1], raw_sig.at[2], raw_mass, raw_strength, raw_mask]
     west_tile = jnp.zeros((DEEP, LANES), f32)
     east_tile = jnp.zeros((DEEP, LANES), f32)
@@ -220,15 +220,15 @@
 
     sides = [
         remote(low, strip.at[:, far, centre], h_send.at[0], h_recv.at[0], at(-1, 0)),
-        remote(high, strip.at[:, near, centre], h_send.at[1], h_recv.at[1], at(1, 0)),
+        remote(high, strip.at[:, near, centre], h_send.at[0], h_recv.at[0], at(1, 0)),
     ]
     south = [
-        remote(corner_out.at[0], corner_in.at[NE], h_send.at[2], h_recv.at[2], at(-1, -1)),
-        remote(corner_out.at[1], corner_in.at[NW], h_send.at[3], h_recv.at[3], at(1, -1)),
+        remote(corner_out.at[0], corner_in.at[NE], h_send.at[1], h_recv.at[1], at(-1, -1)),
+        remote(corner_out.at[1], corner_in.at[NW], h_send.at[1], h_recv.at[1], at(1, -1)),
     ]
     north = [
-        remote(corner_out.at[0], corner_in.at[SE], h_send.at[4], h_recv.at[4], at(-1, 1)),
-        remote(corner_out.at[1], corner_in.at[SW], h_send.at[5], h_recv.at[5], at(1, 1)),
+        remote(corner_out.at[0], corner_in.at[SE], h_send.at[2], h_recv.at[2], at(-1, 1)),
+        remote(corner_out.at[1], corner_in.at[SW], h_send.at[2], h_recv.at[2], at(1, 1)),
     ]
     for c in range(G):
         t = bands[:, :, c * C : (c + 1) * C].reshape(4 * B, C).T
@@ -303,21 +303,19 @@
     forward(True)
     forward(False)
     pack8 = pl.ds(0, 8 * DEEP)
+    pair = pl.ds(0, 2)
 
     @pl.when(has_north)
     def _():
         settle(cor.at[pack8], y_recv.at[0])
-        for copy in south:
-            copy.wait_recv()
+        settle(corner_in.at[pair], h_recv.at[1])
 
     @pl.when(has_south)
     def _():
         settle(cor.at[pack8], y_recv.at[1])
-        for copy in north:
-            copy.wait_recv()
-
-    for copy in sides:
-        copy.wait_recv()
+        settle(corner_in.at[pair], h_recv.at[2])
+
+    settle(strip.at[:, :, centre], h_recv.at[0])
     for p, n in skirts:
         prepare_main(p, n)
     for q in range(8):
@@ -485,59 +483,63 @@
                 o_sem.at[0], o_sem.at[1], {"gx": b, "gy": gy},
             ).start()
 
+    outer = gx >= G - hop
+
     def phases(is_low):
         late = list(range(G // 2, G // 2 + G // 4)) if is_low else list(range(G // 2 - G // 4, G // 2))
         early = [b for b in range(G) if b not in late]
         w0, w1 = PAD + late[0] * B, PAD + (late[-1] + 1) * B
-        arrive(early)
-
-        @pl.when(has_south)
-        def _():
-            settle(cor.at[pack8], y_send.at[0])
-            settle(cor.at[skirt], p_recv.at[1])
-
-        @pl.when(has_north)
-        def _():
-            settle(cor.at[pack8], y_send.at[1])
-            settle(cor.at[skirt], p_recv.at[0])
-
-        edges([-1] + early + [G])
-        outer = (
-            [(PAD - DEEP, DEEP, None)] + spans_of(PAD, w0 - DEEP) + spans_of(w1 + DEEP, T) + [(T, DEEP, None)]
-        )
-        rims = ((w0 - DEEP, DEEP), (w1, DEEP))
-
-        def first(h):
-            if h == 0:
-                return outer + [(p, n, None) for p, n in rims]
-            return outer + [(*rims[0], row8 < DEEP - h), (*rims[1], row8 >= h)]
+        def first(h, side):
+            if side == 0:
+                keep = None if h == 0 else row8 < DEEP - h
+                return [(PAD - DEEP, DEEP, None)] + spans_of(PAD, w0 - DEEP) + [(w0 - DEEP, DEEP, keep)]
+            keep = None if h == 0 else row8 >= h
+            return [(w1, DEEP, keep)] + spans_of(w1 + DEEP, T) + [(T, DEEP, None)]
 
         def second(h):
             inside = spans_of(w0, w1)
             if h == 0:
                 return inside
-            return inside + [(*rims[0], row8 >= DEEP - h), (*rims[1], row8 < h)]
+            return inside + [(w0 - DEEP, DEEP, row8 >= DEEP - h), (w1, DEEP, row8 < h)]
 
         totals = [jnp.zeros((DEEP, C), f32)] * ITERS
-        totals[0] = velocity_step(0, first(0), totals[0])
-        for k in range(1, ITERS):
-            stress_step(k == ITERS - 1, first(2 * k - 1))
-            totals[k] = velocity_step(k, first(2 * k), totals[k])
-        order = list(range(G - 1, -1, -1)) if is_low else list(range(G))
-        left = []
-        for b in order:
-            if b in late:
-                left.append((b, 0, B))
-                continue
-            r, n = 0, B
-            if b == late[0] - 1:
-                n -= DEEP
-                left.append((b, n, DEEP))
-            elif b == late[-1] + 1:
-                r, n = DEEP, n - DEEP
-                left.append((b, 0, DEEP))
-            if n:
-                send_rows(b, r, n)
+        left = [(b, 0, B) for b in late]
+        for side in range(2):
+            bs = [b for b in early if (b > late[0]) == bool(side)]
+            arrive(bs)
+
+            @pl.when(has_north if side else has_south)
+            def _():
+                settle(cor.at[pack8], y_send.at[side])
+                settle(cor.at[skirt], p_recv.at[1 - side])
+
+            edges(bs + [G] if side else [-1] + bs)
+            totals[0] = velocity_step(0, first(0, side), totals[0])
+            for k in range(1, ITERS):
+                stress_step(k == ITERS - 1, first(2 * k - 1, side))
+                totals[k] = velocity_step(k, first(2 * k, side), totals[k])
+            ready_rows = []
+            for b in reversed(bs) if side else bs:
+                r, n = 0, B
+                if b == late[0] - 1:
+                    n -= DEEP
+                    left.append((b, n, DEEP))
+                elif b == late[-1] + 1:
+                    r, n = DEEP, n - DEEP
+                    left.append((b, 0, DEEP))
+                if n:
+                    ready_rows.append((b, r, n))
+
+            def send_ready(pieces=tuple(ready_rows)):
+                for piece in pieces:
+                    send_rows(*piece)
+
+            if side == 0:
+                pl.when(jnp.logical_not(outer))(send_ready)
+                later = send_ready
+            else:
+                send_ready()
+                pl.when(outer)(later)
         arrive(late)
         edges(late)
         totals[0] = velocity_step(0, second(0), totals[0])
@@ -567,19 +569,16 @@
     settle(bands.at[:, :, most], f_send.at[0])
     settle(f_out.at[pl.ds(0, G - 1)], f_send.at[1])
     settle(os_out.at[:, :, most], o_sem.at[0])
-    for copy in sides:
-        copy.wait_send()
+    settle(strip.at[:, :, centre], h_send.at[0])
 
     @pl.when(has_south)
     def _():
-        for copy in south:
-            copy.wait_send()
+        settle(corner_in.at[pair], h_send.at[1])
         settle(cor.at[skirt], p_send.at[0])
 
     @pl.when(has_north)
     def _():
-        for copy in north:
-            copy.wait_send()
+        settle(corner_in.at[pair], h_send.at[2])
         settle(cor.at[skirt], p_send.at[1])
 
     settle(partial.at[peers], r_send.at[0])
@@ -638,12 +637,12 @@
             pltpu.VMEM((G + 2, 2 * REACH, LANES), f32),
             pltpu.VMEM((1, LANES), f32),
             pltpu.VMEM((G * Y, 1, LANES), f32),
-            dma((6,)),
+            dma((3,)),
             dma((2,)),
             dma((G,)),
             dma((2,)),
-            dma((6,)),
-            dma((6,)),
+            dma((3,)),
+            dma((3,)),
             dma((2,)),
             dma((2,)),
             dma((2,)),

time: 29.1 us -> 28.6 us (0.983)
  Pallas kernels: 28.4 us -> 27.8 us
    pallas_call x1, Pallas kernels: 27.4 us -> 26.9 us  [local(): pl.pallas_call(functools.partial(kernel, G, Y, R, C, B), out_shape=(pltpu...]
where the time goes in v4:
time: 28.6 us; the launch traced here: 28.5 us
  Pallas kernels  27.8 us (97%)
  between operations  0.64 us (2%)
    pallas_call x1, Pallas kernels, local(): pl.pallas_call(functools.partial(kernel, G, Y, R, C, B), out_shape=(pltpu...  26.9 us
    pallas_call x1, Pallas kernels, local(): pl.pallas_call(store, out_shape=tuple((jax.ShapeDtypeStruct(x.shape, f32)...  0.96 us

profile of v4, /device:TPU:0, one launch (start us, length us, event | category | flops | bytes accessed | tf_op | source)
XLA Modules:
  0.0 28.5 jit_solution(16691480259458274028)
XLA Ops:
  0.6 26.9 %shard_map.93 = (f32[2,256,128]{2,1,0:T(8,128)S(1)}, f32[3,256,128]{2,1,0:T(8,128)S(1)}, f32[4]{0:T(128)S(1)}, f32[2,32,1024]{2,1,0:T(8,128)S(1)}) custom-call(f32[2,256,128]{2,1,0:T(8,128)} %vel_in.1, f32[3,256,128]{2,1,0:T(8,128)} %sig_in.1, f32[256,128]{1,0:T(8,128)} %mass_in.1, f32[256,128]{1,0:T(8,128)} %strength_in.1, s32[256,128]{1,0:T(8,128)} %mask_in.1, ...), custom_call_target="tpu_custom_call" | custom-call | tf_op jit(solution)/shard_map/pallas_call | solution.py:605
  27.5 1.0 %shard_map.94 = (f32[2,256,128]{2,1,0:T(8,128)}, f32[3,256,128]{2,1,0:T(8,128)}, f32[4]{0:T(128)}, f32[2,32,1024]{2,1,0:T(8,128)}) custom-call(f32[2,256,128]{2,1,0:T(8,128)S(1)} %get-tuple-element.8.vel, f32[3,256,128]{2,1,0:T(8,128)S(1)} %get-tuple-element.9.sig, f32[4]{0:T(128)S(1)} %get-tuple-element.10.res, f32[2,32,1024]{2,1,0:T(8,128)S(1)} %get-tuple-element.11.ocean), custom_call_target="tpu_custom_call" | custom-call | tf_op jit(solution)/shard_map/pallas_call | solution.py:657

commit v5 on v4

--- a/solution.py
+++ b/solution.py
@@ -548,11 +548,13 @@
             totals[k] = velocity_step(k, second(2 * k), totals[k], True)
         answer = jnp.zeros((1, LANES), f32)
         for k in range(ITERS):
-            answer = jnp.where(lane1 == k, jnp.sum(totals[k]), answer)
+            answer = jnp.where(lane1 == k, jnp.sum(jnp.sum(totals[k], axis=0, keepdims=True), axis=1, keepdims=True), answer)
         sums[...] = answer
         me = gx * Y + gy
-        for dx, dy in partners:
-            remote(sums, partial.at[me], r_send.at[0], r_recv.at[0], at(dx, dy)).start()
+        for j in range(len(partners)):
+            peer = j + (j >= me).astype(jnp.int32)
+            where = {"gx": lax.div(peer, Y), "gy": lax.rem(peer, Y)}
+            remote(sums, partial.at[me], r_send.at[0], r_recv.at[0], where).start()
         partial[me] = answer
         for b, r, n in left:
             send_rows(b, r, n)

time: 28.6 us -> 28.5 us (level)
  no operation moved by 1% of the time
where the time goes in v5:
time: 28.5 us; the launch traced here: 28.3 us
  Pallas kernels  27.7 us (97%)
  between operations  0.64 us (2%)
    pallas_call x1, Pallas kernels, local(): pl.pallas_call(functools.partial(kernel, G, Y, R, C, B), out_shape=(pltpu...  26.7 us
    pallas_call x1, Pallas kernels, local(): pl.pallas_call(store, out_shape=tuple((jax.ShapeDtypeStruct(x.shape, f32)...  0.96 us

profile of v5, /device:TPU:0, one launch (start us, length us, event | category | flops | bytes accessed | tf_op | source)
XLA Modules:
  0.0 28.3 jit_solution(11050596685973942038)
XLA Ops:
  0.6 26.7 %shard_map.93 = (f32[2,256,128]{2,1,0:T(8,128)S(1)}, f32[3,256,128]{2,1,0:T(8,128)S(1)}, f32[4]{0:T(128)S(1)}, f32[2,32,1024]{2,1,0:T(8,128)S(1)}) custom-call(f32[2,256,128]{2,1,0:T(8,128)} %vel_in.1, f32[3,256,128]{2,1,0:T(8,128)} %sig_in.1, f32[256,128]{1,0:T(8,128)} %mass_in.1, f32[256,128]{1,0:T(8,128)} %strength_in.1, s32[256,128]{1,0:T(8,128)} %mask_in.1, ...), custom_call_target="tpu_custom_call" | custom-call | tf_op jit(solution)/shard_map/pallas_call | solution.py:607
  27.4 1.0 %shard_map.94 = (f32[2,256,128]{2,1,0:T(8,128)}, f32[3,256,128]{2,1,0:T(8,128)}, f32[4]{0:T(128)}, f32[2,32,1024]{2,1,0:T(8,128)}) custom-call(f32[2,256,128]{2,1,0:T(8,128)S(1)} %get-tuple-element.8.vel, f32[3,256,128]{2,1,0:T(8,128)S(1)} %get-tuple-element.9.sig, f32[4]{0:T(128)S(1)} %get-tuple-element.10.res, f32[2,32,1024]{2,1,0:T(8,128)S(1)} %get-tuple-element.11.ocean), custom_call_target="tpu_custom_call" | custom-call | tf_op jit(solution)/shard_map/pallas_call | solution.py:659

commit v6 on v5

--- a/solution.py
+++ b/solution.py
@@ -223,12 +223,12 @@
         remote(high, strip.at[:, near, centre], h_send.at[0], h_recv.at[0], at(1, 0)),
     ]
     south = [
-        remote(corner_out.at[0], corner_in.at[NE], h_send.at[1], h_recv.at[1], at(-1, -1)),
-        remote(corner_out.at[1], corner_in.at[NW], h_send.at[1], h_recv.at[1], at(1, -1)),
+        remote(corner_out.at[0], corner_in.at[NE], y_send.at[0], y_recv.at[0], at(-1, -1)),
+        remote(corner_out.at[1], corner_in.at[NW], y_send.at[0], y_recv.at[0], at(1, -1)),
     ]
     north = [
-        remote(corner_out.at[0], corner_in.at[SE], h_send.at[2], h_recv.at[2], at(-1, 1)),
-        remote(corner_out.at[1], corner_in.at[SW], h_send.at[2], h_recv.at[2], at(1, 1)),
+        remote(corner_out.at[0], corner_in.at[SE], y_send.at[1], y_recv.at[1], at(-1, 1)),
+        remote(corner_out.at[1], corner_in.at[SW], y_send.at[1], y_recv.at[1], at(1, 1)),
     ]
     for c in range(G):
         t = bands[:, :, c * C : (c + 1) * C].reshape(4 * B, C).T
@@ -302,18 +302,15 @@
 
     forward(True)
     forward(False)
-    pack8 = pl.ds(0, 8 * DEEP)
-    pair = pl.ds(0, 2)
+    pack8 = pl.ds(0, 8 * DEEP + 2 * DEEP)
 
     @pl.when(has_north)
     def _():
         settle(cor.at[pack8], y_recv.at[0])
-        settle(corner_in.at[pair], h_recv.at[1])
 
     @pl.when(has_south)
     def _():
         settle(cor.at[pack8], y_recv.at[1])
-        settle(corner_in.at[pair], h_recv.at[2])
 
     settle(strip.at[:, :, centre], h_recv.at[0])
     for p, n in skirts:
@@ -575,12 +572,10 @@
 
     @pl.when(has_south)
     def _():
-        settle(corner_in.at[pair], h_send.at[1])
         settle(cor.at[skirt], p_send.at[0])
 
     @pl.when(has_north)
     def _():
-        settle(corner_in.at[pair], h_send.at[2])
         settle(cor.at[skirt], p_send.at[1])
 
     settle(partial.at[peers], r_send.at[0])
@@ -643,8 +638,8 @@
             dma((2,)),
             dma((G,)),
             dma((2,)),
-            dma((3,)),
-            dma((3,)),
+            dma((1,)),
+            dma((1,)),
             dma((2,)),
             dma((2,)),
             dma((2,)),

time: 28.5 us -> 28.5 us (level)
  no operation moved by 1% of the time
where the time goes in v6:
time: 28.5 us; the launch traced here: 28.3 us
  Pallas kernels  27.7 us (97%)
  between operations  0.64 us (2%)
    pallas_call x1, Pallas kernels, local(): pl.pallas_call(functools.partial(kernel, G, Y, R, C, B), out_shape=(pltpu...  26.7 us
    pallas_call x1, Pallas kernels, local(): pl.pallas_call(store, out_shape=tuple((jax.ShapeDtypeStruct(x.shape, f32)...  0.96 us

profile of v6, /device:TPU:0, one launch (start us, length us, event | category | flops | bytes accessed | tf_op | source)
XLA Modules:
  0.0 28.3 jit_solution(5242205144886294970)
XLA Ops:
  0.6 26.7 %shard_map.93 = (f32[2,256,128]{2,1,0:T(8,128)S(1)}, f32[3,256,128]{2,1,0:T(8,128)S(1)}, f32[4]{0:T(128)S(1)}, f32[2,32,1024]{2,1,0:T(8,128)S(1)}) custom-call(f32[2,256,128]{2,1,0:T(8,128)} %vel_in.1, f32[3,256,128]{2,1,0:T(8,128)} %sig_in.1, f32[256,128]{1,0:T(8,128)} %mass_in.1, f32[256,128]{1,0:T(8,128)} %strength_in.1, s32[256,128]{1,0:T(8,128)} %mask_in.1, ...), custom_call_target="tpu_custom_call" | custom-call | tf_op jit(solution)/shard_map/pallas_call | solution.py:602
  27.4 1.0 %shard_map.94 = (f32[2,256,128]{2,1,0:T(8,128)}, f32[3,256,128]{2,1,0:T(8,128)}, f32[4]{0:T(128)}, f32[2,32,1024]{2,1,0:T(8,128)}) custom-call(f32[2,256,128]{2,1,0:T(8,128)S(1)} %get-tuple-element.8.vel, f32[3,256,128]{2,1,0:T(8,128)S(1)} %get-tuple-element.9.sig, f32[4]{0:T(128)S(1)} %get-tuple-element.10.res, f32[2,32,1024]{2,1,0:T(8,128)S(1)} %get-tuple-element.11.ocean), custom_call_target="tpu_custom_call" | custom-call | tf_op jit(solution)/shard_map/pallas_call | solution.py:654
